TPU v7x, 32 devices: a whole 2x2x4 slice. The times are simulated.
32 devices in a mesh: depth: 16 (over z, y, x), spec: 2 (over core).
Axes of the slice: x: 2, y: 2, z: 4, core: 2. Of those that a mesh axis runs over, the one named last changes fastest.
Arguments:
- emission: bfloat16 [512, 64, 2048], P('depth', 'spec'), may hold values from 0.099609375 to 2
- opacity: bfloat16 [512, 64, 2048], P('depth', 'spec'), may hold values from 0.29882812 to 3
- bin_extinction: float32 [64], P('spec'), may hold values from 0.1 to 30
- entry: int32 [2048], replicated, may hold values from 0 to 127
- exit_cell: int32 [2048], replicated, may hold values from 384 to 512
- response: float32 [3, 64], P(None, 'spec'), may hold values from 0.05 to 1
Outputs:
- nearer_slab_rgb: float32 [16, 3, 2048], P('depth')
- image: float32 [3, 2048], replicated
All inputs are finite; a program needn't handle non-finite values.
Results may differ from a plain program's by a relative error of at most 0.0003.
Values sent between devices are 32-bit elements; how exact they have to be, the bound alone decides.
A program may use at most 64 MiB of HBM per device.

v0:
```python
import jax
import jax.numpy as jnp
from jax import lax
from jax.sharding import PartitionSpec as P


def merge_slabs(earlier, later):
    return (earlier[0] + earlier[1] * later[0], earlier[1] * later[1])


def body(emission, opacity, bin_extinction, entry, exit_cell, response):
    cells = emission.shape[0]
    sections = lax.axis_size("depth")
    cell_step = 1.0 / (cells * sections)
    depth = lax.axis_index("depth") * cells + jnp.arange(cells, dtype=jnp.int32)
    inside = (depth[:, None] >= entry[None, :]) & (depth[:, None] < exit_cell[None, :])
    live = jnp.where(inside, 1.0, 0.0).astype(jnp.float32)
    tau = bin_extinction[None, :, None] * opacity.astype(jnp.float32) * live[:, None, :] * cell_step
    rows = jnp.arange(cells, dtype=jnp.int32)
    lower = jnp.where(rows[None, :] < rows[:, None], 1.0, 0.0).astype(jnp.float32)
    before = jnp.einsum("ij,jbr->ibr", lower, tau, precision=lax.Precision.HIGHEST)
    light = jnp.sum(
        emission.astype(jnp.float32) * live[:, None, :] * cell_step * jnp.exp(-before), axis=0
    )
    trans = jnp.exp(-jnp.sum(tau, axis=0))
    pieces = (
        lax.all_to_all(light[None], "depth", split_axis=2, concat_axis=0, tiled=True),
        lax.all_to_all(trans[None], "depth", split_axis=2, concat_axis=0, tiled=True),
    )
    totals = lax.associative_scan(merge_slabs, (pieces[0], pieces[1]), axis=0)
    lead_light = jnp.concatenate([jnp.zeros_like(pieces[0][:1]), totals[0][:-1]], axis=0)
    lead_trans = jnp.concatenate([jnp.ones_like(pieces[1][:1]), totals[1][:-1]], axis=0)
    moved_light = lax.all_to_all(lead_light, "depth", split_axis=0, concat_axis=2, tiled=True)
    moved_trans = lax.all_to_all(lead_trans, "depth", split_axis=0, concat_axis=2, tiled=True)
    nearer_radiance = moved_light[0]
    nearer_transparency = moved_trans[0]
    front_part = jnp.dot(response, nearer_radiance, precision=lax.Precision.HIGHEST)
    slab_portion = jnp.dot(response, nearer_transparency * light, precision=lax.Precision.HIGHEST)
    nearer_slab_rgb, slab_colour_rgb = lax.psum((front_part, slab_portion), "spec")
    image = lax.psum(slab_colour_rgb, "depth")
    return (nearer_slab_rgb[None], image)


def solution(mesh):
    placed = (
        P("depth", "spec", None),
        P("depth", "spec", None),
        P("spec"),
        P(),
        P(),
        P(None, "spec"),
    )
    return jax.shard_map(
        body, mesh=mesh, in_specs=placed, out_specs=(P("depth", None, None), P()), check_vma=False
    )
```

profile of v0, /device:TPU:0, one launch (start us, length us, event | category | flops | bytes accessed | tf_op | source)
XLA Modules:
  0.0 190.8 jit_solution(17573433646198136472)
XLA Ops:
  0.7 0.8 and_select_fusion
  1.5 5.9 %fusion = f32[32,2048]{1,0:T(8,128)S(1)} fusion(f32[32]{0:T(128)} %param.8, f32[32,2048]{1,0:T(8,128)S(1)} %and_select_fusion, bf16[32,32,2048]{2,1,0:T(8,128)(2,1)} %param.7), kind=kLoop, calls=%fused_computation.2 | loop fusion | flops 10420224 | bytes 4718720 | tf_op jit(solution)/shard_map/reduce_sum | solution.py:25
  7.4 0.6 copy.48
  8.0 0.5 broadcast.88
  8.5 9.3 %reduce = f32[2048,32]{1,0:T(8,128)S(1)} reduce(f32[2048,1,32]{2,1,0:T(1,128)S(1)} %bitcast.63, f32[]{:T(128)} %broadcast.88), dimensions={1}, to_apply=%bitcast.47.reduce_sub_computation | reduce | bytes 524292
  17.9 1.1 reshape.76
  19.0 8.3 %all-to-all-start.1 = ((f32[16,1,4096]{2,1,0:T(1,128)}), f32[16,1,4096]{2,1,0:T(1,128)S(1)}, u32[]{:S(2)}, u32[]{:S(2)}) async-start(f32[16,1,4096]{2,1,0:T(1,128)} %reshape.76), calls=%async_computation.1 | async-start | bytes 524288 | tf_op jit(solution)/shard_map/all_to_all | solution.py:28
  27.4 21.2 %multiply_reduce_fusion = f32[32,2048]{1,0:T(8,128)S(1)} fusion(bf16[32,32,2048]{2,1,0:T(8,128)(2,1)} %param.6, f32[32]{0:T(128)S(1)} %copy-done.1, f32[32,2048]{1,0:T(8,128)S(1)} %and_select_fusion, bf16[32,32,2048]{2,1,0:T(8,128)(2,1)} %param.7), kind=kOutput, calls=%fused_computation | convolution fusion | flops 826214400 | bytes 8913024 | tf_op jit(solution)/shard_map/ij,jbr->ibr/dot_general | solution.py:21
  48.6 0.6 copy.46
  49.2 9.6 %reduce.2 = f32[2048,32]{1,0:T(8,128)S(1)} reduce(f32[2048,1,32]{2,1,0:T(1,128)S(1)} %bitcast.66, f32[]{:T(128)} %broadcast.88), dimensions={1}, to_apply=%bitcast.45.reduce_sub_computation | reduce | bytes 524292
  58.8 1.2 reshape.74
  59.9 6.9 %all-to-all-start = ((f32[16,1,4096]{2,1,0:T(1,128)}), f32[16,1,4096]{2,1,0:T(1,128)S(1)}, u32[]{:S(2)}, u32[]{:S(2)}) async-start(f32[16,1,4096]{2,1,0:T(1,128)} %reshape.74), calls=%async_computation | async-start | bytes 524288 | tf_op jit(solution)/shard_map/all_to_all | solution.py:27
  66.8 1.3 reduce.1
  68.1 1.8 reshape.77
  69.9 0.6 copy.49
  70.9 5.3 %all-to-all-done = f32[16,1,4096]{2,1,0:T(1,128)S(1)} async-done(((f32[16,1,4096]{2,1,0:T(1,128)}), f32[16,1,4096]{2,1,0:T(1,128)S(1)}, u32[]{:S(2)}, u32[]{:S(2)}) %all-to-all-start) | async-done | bytes 262176 | tf_op jit(solution)/shard_map/all_to_all | solution.py:27
  76.2 1.3 reduce.3
  77.4 1.8 reshape.75
  79.3 0.3 copy.57
  80.7 0.1 slice.138
  80.8 0.1 slice.135
  80.9 0.1 slice.133
  81.0 0.1 slice.136
  81.5 0.4 pad.59
  81.9 0.4 pad.58
  82.4 0.4 pad.56
  82.8 0.4 pad.57
  83.4 0.2 pad.60
  83.7 0.2 pad.62
  83.9 0.2 pad.63
  84.1 0.2 pad.61
  84.5 0.2 pad.84
  84.8 0.2 pad.125
  85.2 0.7 concatenate.31.clone
  85.9 3.5 %all-to-all-start.3 = ((f32[16,32,128]{2,1,0:T(8,128)}), f32[16,32,128]{2,1,0:T(8,128)S(1)}, u32[]{:S(2)}, u32[]{:S(2)}) async-start(f32[16,32,128]{2,1,0:T(8,128)} %concatenate.31.clone), calls=%async_computation.3 | async-start | bytes 524288 | tf_op jit(solution)/shard_map/all_to_all | solution.py:34
  89.5 0.2 pad.82
  89.7 0.2 pad.124
  90.1 0.7 concatenate.29.clone
  90.8 7.8 %all-to-all-done.3 = f32[16,32,128]{2,1,0:T(8,128)S(1)} async-done(((f32[16,32,128]{2,1,0:T(8,128)}), f32[16,32,128]{2,1,0:T(8,128)S(1)}, u32[]{:S(2)}, u32[]{:S(2)}) %all-to-all-start.3) | async-done | bytes 262176 | tf_op jit(solution)/shard_map/all_to_all | solution.py:34
  98.7 3.5 %all-to-all-start.2 = ((f32[16,32,128]{2,1,0:T(8,128)}), f32[16,32,128]{2,1,0:T(8,128)S(1)}, u32[]{:S(2)}, u32[]{:S(2)}) async-start(f32[16,32,128]{2,1,0:T(8,128)} %concatenate.29.clone), calls=%async_computation.2 | async-start | bytes 524288 | tf_op jit(solution)/shard_map/all_to_all | solution.py:33
  102.2 0.2 copy.55
  102.4 9.0 %all-to-all-done.2 = f32[16,32,128]{2,1,0:T(8,128)S(1)} async-done(((f32[16,32,128]{2,1,0:T(8,128)}), f32[16,32,128]{2,1,0:T(8,128)S(1)}, u32[]{:S(2)}, u32[]{:S(2)}) %all-to-all-start.2) | async-done | bytes 262176 | tf_op jit(solution)/shard_map/all_to_all | solution.py:33
  111.4 0.2 copy.52
  111.5 0.3 convolution_bitcast_fusion
  111.9 0.3 convolution_bitcast_fusion.1
  112.2 3.6 %all-reduce.18 = (f32[1,3,2048]{2,1,0:T(4,128)S(1)}, f32[3,2048]{1,0:T(4,128)S(1)}) all-reduce(f32[1,3,2048]{2,1,0:T(4,128)S(1)} %convolution_bitcast_fusion.1, f32[3,2048]{1,0:T(4,128)S(1)} %convolution_bitcast_fusion), channel_id=1, replica_groups=mesh['depth'=16,'spec'=2] {'spec'}, use_global_device_ids=true, to_apply=%region_2.3 | all-reduce | flops 12288 | bytes 98304 | tf_op jit(solution)/shard_map/psum | solution.py:39
  115.8 0.6 copy.56
  116.5 74.4 %psum.23 = f32[3,2048]{1,0:T(4,128)} all-reduce(f32[3,2048]{1,0:T(4,128)S(1)} %get-tuple-element.13), channel_id=1, replica_groups=mesh['depth'=16,'spec'=2] {'depth'}, use_global_device_ids=true, to_apply=%region_4.5 | all-reduce | flops 6144 | bytes 49152 | tf_op jit(solution)/shard_map/psum | solution.py:40
  (45 shorter events, 2.2 us)
Async XLA Ops:
  0.6 110.9 %copy-start = (f32[3,32]{1,0:T(4,128)S(1)}, f32[3,32]{1,0:T(4,128)}, u32[]{:S(2)}) copy-start(f32[3,32]{1,0:T(4,128)} %param.11) | copy-start | bytes 1156
  1.5 25.9 %copy-start.1 = (f32[32]{0:T(128)S(1)}, f32[32]{0:T(128)}, u32[]{:S(2)}) copy-start(f32[32]{0:T(128)} %param.8) | copy-start | bytes 388
  19.0 40.9 %all-to-all-start.1 = ((f32[16,1,4096]{2,1,0:T(1,128)}), f32[16,1,4096]{2,1,0:T(1,128)S(1)}, u32[]{:S(2)}, u32[]{:S(2)}) async-start(f32[16,1,4096]{2,1,0:T(1,128)} %reshape.76), calls=%async_computation.1 | async-start | bytes 524288 | tf_op jit(solution)/shard_map/all_to_all | solution.py:28
  59.9 16.2 %all-to-all-start = ((f32[16,1,4096]{2,1,0:T(1,128)}), f32[16,1,4096]{2,1,0:T(1,128)S(1)}, u32[]{:S(2)}, u32[]{:S(2)}) async-start(f32[16,1,4096]{2,1,0:T(1,128)} %reshape.74), calls=%async_computation | async-start | bytes 524288 | tf_op jit(solution)/shard_map/all_to_all | solution.py:27
  85.9 12.8 %all-to-all-start.3 = ((f32[16,32,128]{2,1,0:T(8,128)}), f32[16,32,128]{2,1,0:T(8,128)S(1)}, u32[]{:S(2)}, u32[]{:S(2)}) async-start(f32[16,32,128]{2,1,0:T(8,128)} %concatenate.31.clone), calls=%async_computation.3 | async-start | bytes 524288 | tf_op jit(solution)/shard_map/all_to_all | solution.py:34
  98.7 12.7 %all-to-all-start.2 = ((f32[16,32,128]{2,1,0:T(8,128)}), f32[16,32,128]{2,1,0:T(8,128)S(1)}, u32[]{:S(2)}, u32[]{:S(2)}) async-start(f32[16,32,128]{2,1,0:T(8,128)} %concatenate.29.clone), calls=%async_computation.2 | async-start | bytes 524288 | tf_op jit(solution)/shard_map/all_to_all | solution.py:33
where the time goes:
time: 192 us; the launch traced here: 191 us
  blocking collectives  78 us (41%)
  other arithmetic  28.9 us (15%)
  starting transfers between devices  22.3 us (12%)
  waiting for transfers between devices  22.1 us (12%)
  matrix products  21.8 us (11%)
  local copies, waits for them, and re-layouts  16.5 us (9%)
    psum x1, blocking collectives, body(): image = lax.psum(slab_colour_rgb, 'depth')  74.4 us
    dot_general x1, matrix products, body(): jnp.einsum('ij,jbr->ibr', lower, tau, precision=lax.Precision.HIGHEST)  21.2 us
    unnamed x2, other arithmetic  18.9 us
    all_to_all x1, waiting for transfers between devices, body(): lax.all_to_all(lead_light, 'depth', split_axis=0, concat_axis=2, tiled=True)  8.99 us
    all_to_all x1, starting transfers between devices, body(): lax.all_to_all(trans[None], 'depth', split_axis=2, concat_axis=0, tiled=T...  8.35 us
    all_to_all x1, waiting for transfers between devices, body(): lax.all_to_all(lead_trans, 'depth', split_axis=0, concat_axis=2, tiled=True)  7.84 us
    unnamed x14, local copies, waits for them, and re-layouts  7.74 us
    all_to_all x1, starting transfers between devices, body(): lax.all_to_all(light[None], 'depth', split_axis=2, concat_axis=0, tiled=T...  6.9 us
  transfers between devices with their start and end apart: 4, of which 3 were waited for; matrix products, arithmetic and copies ran while one was open for 20% of the time, Pallas kernels for 0%

commit v1 on v0

--- a/solution.py
+++ b/solution.py
@@ -37,7 +37,10 @@
     front_part = jnp.dot(response, nearer_radiance, precision=lax.Precision.HIGHEST)
     slab_portion = jnp.dot(response, nearer_transparency * light, precision=lax.Precision.HIGHEST)
     nearer_slab_rgb, slab_colour_rgb = lax.psum((front_part, slab_portion), "spec")
-    image = lax.psum(slab_colour_rgb, "depth")
+    devices, image = (lax.axis_size("depth"), slab_colour_rgb)
+    for hop in [1 << k for k in range(devices.bit_length() - 1)]:
+        swap = [(i, i ^ hop) for i in range(devices)]
+        image = image + lax.ppermute(image, "depth", swap)
     return (nearer_slab_rgb[None], image)
 
 

time: 192 us -> 134 us (0.70)
  blocking collectives: 78 us -> 3.6 us
  waiting for transfers between devices: 22.1 us -> 34.5 us
  starting transfers between devices: 22.3 us -> 26.1 us
    psum x1 -> x0, blocking collectives: 74.4 us -> none  [body(): image = lax.psum(slab_colour_rgb, 'depth')]
    ppermute x0 -> x4, waiting for transfers between devices: none -> 12.4 us  [body(): image = image + lax.ppermute(image, 'depth', swap)]
    ppermute x0 -> x4, starting transfers between devices: none -> 3.77 us  [body(): image = image + lax.ppermute(image, 'depth', swap)]
  transfers between devices with their start and end apart: 4 -> 8, of which waited for: 3 -> 7; matrix products, arithmetic and copies ran while one was open for 20% -> 29% of each run, Pallas kernels for 0% -> 0%
where the time goes in v1:
time: 134 us; the launch traced here: 133 us
  waiting for transfers between devices  34.5 us (26%)
  other arithmetic  29.6 us (22%)
  starting transfers between devices  26.1 us (19%)
  matrix products  21.8 us (16%)
  local copies, waits for them, and re-layouts  16.5 us (12%)
  blocking collectives  3.6 us (3%)
    dot_general x1, matrix products, body(): jnp.einsum('ij,jbr->ibr', lower, tau, precision=lax.Precision.HIGHEST)  21.2 us
    unnamed x2, other arithmetic  18.9 us
    ppermute x4, waiting for transfers between devices, body(): image = image + lax.ppermute(image, 'depth', swap)  12.4 us
    all_to_all x1, waiting for transfers between devices, body(): lax.all_to_all(lead_light, 'depth', split_axis=0, concat_axis=2, tiled=True)  8.98 us
    all_to_all x1, starting transfers between devices, body(): lax.all_to_all(trans[None], 'depth', split_axis=2, concat_axis=0, tiled=T...  8.35 us
    all_to_all x1, waiting for transfers between devices, body(): lax.all_to_all(lead_trans, 'depth', split_axis=0, concat_axis=2, tiled=True)  7.84 us
    unnamed x14, local copies, waits for them, and re-layouts  7.74 us
    all_to_all x1, starting transfers between devices, body(): lax.all_to_all(light[None], 'depth', split_axis=2, concat_axis=0, tiled=T...  6.88 us
  transfers between devices with their start and end apart: 8, of which 7 were waited for; matrix products, arithmetic and copies ran while one was open for 29% of the time, Pallas kernels for 0%

profile of v1, /device:TPU:0, one launch (start us, length us, event | category | flops | bytes accessed | tf_op | source)
XLA Modules:
  0.0 133.3 jit_solution(9755418094442120630)
XLA Ops:
  0.7 0.8 and_select_fusion
  1.5 5.9 %fusion = f32[32,2048]{1,0:T(8,128)S(1)} fusion(f32[32]{0:T(128)} %param.8, f32[32,2048]{1,0:T(8,128)S(1)} %and_select_fusion, bf16[32,32,2048]{2,1,0:T(8,128)(2,1)} %param.7), kind=kLoop, calls=%fused_computation.2 | loop fusion | flops 10420224 | bytes 4718720 | tf_op jit(solution)/shard_map/reduce_sum | solution.py:25
  7.4 0.6 copy.48
  8.0 0.5 broadcast.88
  8.5 9.3 %reduce = f32[2048,32]{1,0:T(8,128)S(1)} reduce(f32[2048,1,32]{2,1,0:T(1,128)S(1)} %bitcast.63, f32[]{:T(128)} %broadcast.88), dimensions={1}, to_apply=%bitcast.47.reduce_sub_computation | reduce | bytes 524292
  17.9 1.1 reshape.76
  19.0 8.3 %all-to-all-start.1 = ((f32[16,1,4096]{2,1,0:T(1,128)}), f32[16,1,4096]{2,1,0:T(1,128)S(1)}, u32[]{:S(2)}, u32[]{:S(2)}) async-start(f32[16,1,4096]{2,1,0:T(1,128)} %reshape.76), calls=%async_computation.1 | async-start | bytes 524288 | tf_op jit(solution)/shard_map/all_to_all | solution.py:28
  27.4 21.2 %multiply_reduce_fusion = f32[32,2048]{1,0:T(8,128)S(1)} fusion(bf16[32,32,2048]{2,1,0:T(8,128)(2,1)} %param.6, f32[32]{0:T(128)S(1)} %copy-done.1, f32[32,2048]{1,0:T(8,128)S(1)} %and_select_fusion, bf16[32,32,2048]{2,1,0:T(8,128)(2,1)} %param.7), kind=kOutput, calls=%fused_computation | convolution fusion | flops 826214400 | bytes 8913024 | tf_op jit(solution)/shard_map/ij,jbr->ibr/dot_general | solution.py:21
  48.6 0.6 copy.46
  49.2 9.6 %reduce.2 = f32[2048,32]{1,0:T(8,128)S(1)} reduce(f32[2048,1,32]{2,1,0:T(1,128)S(1)} %bitcast.66, f32[]{:T(128)} %broadcast.88), dimensions={1}, to_apply=%bitcast.45.reduce_sub_computation | reduce | bytes 524292
  58.8 1.2 reshape.74
  59.9 6.9 %all-to-all-start = ((f32[16,1,4096]{2,1,0:T(1,128)}), f32[16,1,4096]{2,1,0:T(1,128)S(1)}, u32[]{:S(2)}, u32[]{:S(2)}) async-start(f32[16,1,4096]{2,1,0:T(1,128)} %reshape.74), calls=%async_computation | async-start | bytes 524288 | tf_op jit(solution)/shard_map/all_to_all | solution.py:27
  66.8 1.3 reduce.1
  68.1 1.8 %reshape.77 = f32[2048,1,32]{2,1,0:T(1,128)S(1)} reshape(f32[16,4096]{1,0:T(8,128)S(1)} %reduce.1) | data formatting | bytes 524288
  69.9 0.6 copy.49
  70.9 5.3 %all-to-all-done = f32[16,1,4096]{2,1,0:T(1,128)S(1)} async-done(((f32[16,1,4096]{2,1,0:T(1,128)}), f32[16,1,4096]{2,1,0:T(1,128)S(1)}, u32[]{:S(2)}, u32[]{:S(2)}) %all-to-all-start) | async-done | bytes 262176 | tf_op jit(solution)/shard_map/all_to_all | solution.py:27
  76.1 1.3 reduce.3
  77.4 1.8 %reshape.75 = f32[2048,1,32]{2,1,0:T(1,128)S(1)} reshape(f32[16,4096]{1,0:T(8,128)S(1)} %reduce.3) | data formatting | bytes 524288
  79.3 0.3 copy.57
  81.5 0.4 pad.59
  81.9 0.4 pad.58
  82.4 0.4 pad.56
  82.8 0.4 pad.57
  83.4 0.2 pad.60
  83.6 0.2 pad.62
  83.9 0.2 pad.63
  84.1 0.2 pad.61
  84.5 0.2 pad.84
  84.8 0.2 pad.125
  85.1 0.7 concatenate.31.clone
  85.9 3.5 %all-to-all-start.3 = ((f32[16,32,128]{2,1,0:T(8,128)}), f32[16,32,128]{2,1,0:T(8,128)S(1)}, u32[]{:S(2)}, u32[]{:S(2)}) async-start(f32[16,32,128]{2,1,0:T(8,128)} %concatenate.31.clone), calls=%async_computation.3 | async-start | bytes 524288 | tf_op jit(solution)/shard_map/all_to_all | solution.py:34
  90.1 0.7 concatenate.29.clone
  90.8 7.8 %all-to-all-done.3 = f32[16,32,128]{2,1,0:T(8,128)S(1)} async-done(((f32[16,32,128]{2,1,0:T(8,128)}), f32[16,32,128]{2,1,0:T(8,128)S(1)}, u32[]{:S(2)}, u32[]{:S(2)}) %all-to-all-start.3) | async-done | bytes 262176 | tf_op jit(solution)/shard_map/all_to_all | solution.py:34
  98.7 3.5 %all-to-all-start.2 = ((f32[16,32,128]{2,1,0:T(8,128)}), f32[16,32,128]{2,1,0:T(8,128)S(1)}, u32[]{:S(2)}, u32[]{:S(2)}) async-start(f32[16,32,128]{2,1,0:T(8,128)} %concatenate.29.clone), calls=%async_computation.2 | async-start | bytes 524288 | tf_op jit(solution)/shard_map/all_to_all | solution.py:33
  102.4 9.0 %all-to-all-done.2 = f32[16,32,128]{2,1,0:T(8,128)S(1)} async-done(((f32[16,32,128]{2,1,0:T(8,128)}), f32[16,32,128]{2,1,0:T(8,128)S(1)}, u32[]{:S(2)}, u32[]{:S(2)}) %all-to-all-start.2) | async-done | bytes 262176 | tf_op jit(solution)/shard_map/all_to_all | solution.py:33
  111.5 0.3 convolution_bitcast_fusion
  111.9 0.3 convolution_bitcast_fusion.1
  112.2 3.6 %all-reduce.18 = (f32[1,3,2048]{2,1,0:T(4,128)S(1)}, f32[3,2048]{1,0:T(4,128)S(1)}) all-reduce(f32[1,3,2048]{2,1,0:T(4,128)S(1)} %convolution_bitcast_fusion.1, f32[3,2048]{1,0:T(4,128)S(1)} %convolution_bitcast_fusion), channel_id=1, replica_groups=mesh['depth'=16,'spec'=2] {'spec'}, use_global_device_ids=true, to_apply=%region_2.3 | all-reduce | flops 12288 | bytes 98304 | tf_op jit(solution)/shard_map/psum | solution.py:39
  115.8 0.9 collective-permute-start
  116.6 3.1 %collective-permute-done = f32[3,2048]{1,0:T(4,128)S(1)} collective-permute-done((f32[3,2048]{1,0:T(4,128)S(1)}, f32[3,2048]{1,0:T(4,128)S(1)}, u32[]{:S(2)}, u32[]{:S(2)}) %collective-permute-start) | collective-permute-done | bytes 24608 | tf_op jit(solution)/shard_map/ppermute | solution.py:43
  119.8 1.0 collective-permute-start.1
  120.8 3.0 %collective-permute-done.1 = f32[3,2048]{1,0:T(4,128)S(1)} collective-permute-done((f32[3,2048]{1,0:T(4,128)S(1)}, f32[3,2048]{1,0:T(4,128)S(1)}, u32[]{:S(2)}, u32[]{:S(2)}) %collective-permute-start.1) | collective-permute-done | bytes 24608 | tf_op jit(solution)/shard_map/ppermute | solution.py:43
  123.8 1.2 collective-permute-start.2
  124.9 2.8 %collective-permute-done.2 = f32[3,2048]{1,0:T(4,128)S(1)} collective-permute-done((f32[3,2048]{1,0:T(4,128)S(1)}, f32[3,2048]{1,0:T(4,128)S(1)}, u32[]{:S(2)}, u32[]{:S(2)}) %collective-permute-start.2) | collective-permute-done | bytes 24608 | tf_op jit(solution)/shard_map/ppermute | solution.py:43
  127.8 0.8 collective-permute-start.3
  128.6 0.6 copy.56
  129.2 3.5 %collective-permute-done.3 = f32[3,2048]{1,0:T(4,128)S(1)} collective-permute-done((f32[3,2048]{1,0:T(4,128)S(1)}, f32[3,2048]{1,0:T(4,128)S(1)}, u32[]{:S(2)}, u32[]{:S(2)}) %collective-permute-start.3) | collective-permute-done | bytes 24608 | tf_op jit(solution)/shard_map/ppermute | solution.py:43
  132.7 0.6 add.127
  (56 shorter events, 3.4 us)
Async XLA Ops:
  0.6 110.9 %copy-start = (f32[3,32]{1,0:T(4,128)S(1)}, f32[3,32]{1,0:T(4,128)}, u32[]{:S(2)}) copy-start(f32[3,32]{1,0:T(4,128)} %param.11) | copy-start | bytes 1156
  1.5 25.9 %copy-start.1 = (f32[32]{0:T(128)S(1)}, f32[32]{0:T(128)}, u32[]{:S(2)}) copy-start(f32[32]{0:T(128)} %param.8) | copy-start | bytes 388
  19.0 40.9 %all-to-all-start.1 = ((f32[16,1,4096]{2,1,0:T(1,128)}), f32[16,1,4096]{2,1,0:T(1,128)S(1)}, u32[]{:S(2)}, u32[]{:S(2)}) async-start(f32[16,1,4096]{2,1,0:T(1,128)} %reshape.76), calls=%async_computation.1 | async-start | bytes 524288 | tf_op jit(solution)/shard_map/all_to_all | solution.py:28
  59.9 16.2 %all-to-all-start = ((f32[16,1,4096]{2,1,0:T(1,128)}), f32[16,1,4096]{2,1,0:T(1,128)S(1)}, u32[]{:S(2)}, u32[]{:S(2)}) async-start(f32[16,1,4096]{2,1,0:T(1,128)} %reshape.74), calls=%async_computation | async-start | bytes 524288 | tf_op jit(solution)/shard_map/all_to_all | solution.py:27
  85.9 12.8 %all-to-all-start.3 = ((f32[16,32,128]{2,1,0:T(8,128)}), f32[16,32,128]{2,1,0:T(8,128)S(1)}, u32[]{:S(2)}, u32[]{:S(2)}) async-start(f32[16,32,128]{2,1,0:T(8,128)} %concatenate.31.clone), calls=%async_computation.3 | async-start | bytes 524288 | tf_op jit(solution)/shard_map/all_to_all | solution.py:34
  98.7 12.7 %all-to-all-start.2 = ((f32[16,32,128]{2,1,0:T(8,128)}), f32[16,32,128]{2,1,0:T(8,128)S(1)}, u32[]{:S(2)}, u32[]{:S(2)}) async-start(f32[16,32,128]{2,1,0:T(8,128)} %concatenate.29.clone), calls=%async_computation.2 | async-start | bytes 524288 | tf_op jit(solution)/shard_map/all_to_all | solution.py:33
  115.8 4.0 %collective-permute-start = (f32[3,2048]{1,0:T(4,128)S(1)}, f32[3,2048]{1,0:T(4,128)S(1)}, u32[]{:S(2)}, u32[]{:S(2)}) collective-permute-start(f32[3,2048]{1,0:T(4,128)S(1)} %get-tuple-element.13), channel_id=1, source_target_pairs={{0,2},{2,0},{4,6},{6,4},{8,10},{10,8},{12,14},{14,12},{16,18},{18,... | collective-permute-start | bytes 73736 | tf_op jit(solution)/shard_map/ppermute | solution.py:43
  119.8 4.0 %collective-permute-start.1 = (f32[3,2048]{1,0:T(4,128)S(1)}, f32[3,2048]{1,0:T(4,128)S(1)}, u32[]{:S(2)}, u32[]{:S(2)}) collective-permute-start(f32[3,2048]{1,0:T(4,128)S(1)} %add.124), channel_id=1, source_target_pairs={{0,4},{2,6},{4,0},{6,2},{8,12},{10,14},{12,8},{14,10},{16,20},{18,... | collective-permute-start | bytes 73736 | tf_op jit(solution)/shard_map/ppermute | solution.py:43
  123.8 4.0 %collective-permute-start.2 = (f32[3,2048]{1,0:T(4,128)S(1)}, f32[3,2048]{1,0:T(4,128)S(1)}, u32[]{:S(2)}, u32[]{:S(2)}) collective-permute-start(f32[3,2048]{1,0:T(4,128)S(1)} %add.125), channel_id=1, source_target_pairs={{0,8},{2,10},{4,12},{6,14},{8,0},{10,2},{12,4},{14,6},{16,24},{18,... | collective-permute-start | bytes 73736 | tf_op jit(solution)/shard_map/ppermute | solution.py:43
  127.8 4.9 %collective-permute-start.3 = (f32[3,2048]{1,0:T(4,128)S(1)}, f32[3,2048]{1,0:T(4,128)S(1)}, u32[]{:S(2)}, u32[]{:S(2)}) collective-permute-start(f32[3,2048]{1,0:T(4,128)S(1)} %add.126), channel_id=1, source_target_pairs={{0,16},{2,18},{4,20},{6,22},{8,24},{10,26},{12,28},{14,30},{16,0},... | collective-permute-start | bytes 73736 | tf_op jit(solution)/shard_map/ppermute | solution.py:43
